TPU v7x, 256 devices: a whole 4x4x8 slice. The times are simulated.
256 devices in a mesh: dp: 256 (over z, x, y, core).
Axes of the slice: x: 4, y: 4, z: 8, core: 2. Of those that a mesh axis runs over, the one named last changes fastest.
Arguments:
- images: bfloat16 [1024, 92, 4096], P('dp'), may hold values from -6 to 6
- layer_gain: float32 [4096], replicated, may hold values from 0.5 to 1.5
- in_weight: bfloat16 [4096, 1024], replicated, may hold values from -1 to 1
- out_weight: bfloat16 [1024, 1024], replicated, may hold values from -1 to 1
- text_embed: bfloat16 [1024, 1024], P('dp'), may hold values from -6 to 6
- pair_index: int32 [1024], P('dp'), may hold values from 0 to 1023, each once
- logit_scale: float32 [1], replicated, may hold values from 30 to 200
Outputs:
- loss: float32 [1], replicated
- grad_norm: float32 [1], replicated
- update_image: float32 [1024, 1024], P('dp')
- update_text: float32 [1024, 1024], P('dp')
Inputs may be any that keep to these rules, and one draw needn't show every extreme that they name: Image i is paired with text row pair_index[i]; every text row is paired with exactly one image.
All inputs are finite; a program needn't handle non-finite values.
Results may differ from a plain program's by a relative error of at most 0.0086.
Values may be sent and summed in bfloat16 or wider, within the bound.
A program may use at most 64 MiB of HBM per device.

v0:
```python
import jax
import jax.numpy as jnp
from jax import lax
from jax.sharding import Mesh
from jax.sharding import PartitionSpec as P

DP = ("dp_0", "dp_1", "dp_2", "dp_3")


EPS_UNIT = 1e-06
EPS_LAYER = 1e-05


def from_everyone(array, axis):
    size = lax.axis_size(axis)
    return lax.all_to_all(
        jnp.broadcast_to(array[None], (size, *array.shape)), axis, 0, 0, tiled=True
    )


def laid_out(blocks, dim):
    lengths = list(blocks.shape[1:])
    lengths[dim] *= blocks.shape[0]
    return jnp.moveaxis(blocks, 0, dim).reshape(lengths)


def whole_of(array, axes, dim):
    far, near = axes
    first = from_everyone(array, far)
    blocks = jnp.swapaxes(from_everyone(first, near), 0, 1)
    return laid_out(blocks.reshape(-1, *array.shape), dim)


def turned_gather(arrays, axis, dims):
    turned = [jnp.moveaxis(a, dim, 0) for a, dim in zip(arrays, dims)]
    both = jnp.concatenate([t.reshape(len(t), -1) for t in turned], axis=1)
    filled, at, finished = (lax.all_gather(both, axis, axis=0, tiled=True), 0, [])
    for t, dim in zip(turned, dims):
        section = filled[:, at : at + t[0].size].reshape(-1, *t.shape[1:])
        finished.append(jnp.moveaxis(section, 0, dim))
        at += t[0].size
    return tuple(finished)


def over_copies(array, axis):
    return from_everyone(array, axis).sum(axis=0)


def one_axis_at_a_time(array, axes):
    far, near = axes
    return over_copies(over_copies(array, near), far)


def in_one(arrays, axis):
    ends = [0]
    for a in arrays:
        ends.append(ends[-1] + a.size)
    subtotal = one_axis_at_a_time(jnp.concatenate([a.ravel() for a in arrays]), axis)
    return tuple((subtotal[b:e].reshape(a.shape) for a, b, e in zip(arrays, ends, ends[1:])))


def unit_rows(matrix):
    length = jnp.sqrt(jnp.sum(matrix * matrix, axis=1, keepdims=True) + EPS_UNIT)
    return (matrix / length, length)


def unit_backward(grad_unit, unit_vec, length):
    return (grad_unit - unit_vec * jnp.sum(unit_vec * grad_unit, axis=1, keepdims=True)) / length


def per_device(images, layer_gain, in_weight, out_weight, text_embed, pair_index, logit_scale):
    multiplier = logit_scale[0]
    local_rows = images.shape[0]
    devices = lax.axis_size(DP)
    total_rows = local_rows * devices
    width = out_weight.shape[1]
    first_row = lax.axis_index(DP) * local_rows
    text_unit, text_len = unit_rows(text_embed.astype(jnp.float32))
    text_vec = text_unit.astype(jnp.bfloat16)
    all_text = whole_of(text_vec, (("dp_0", "dp_1"), ("dp_2", "dp_3")), 0)
    values = images.astype(jnp.float32)
    average = jnp.mean(values, axis=-1, keepdims=True)
    centered = values - average
    variance = jnp.mean(centered * centered, axis=-1, keepdims=True)
    normed = (centered * lax.rsqrt(variance + EPS_LAYER) * layer_gain).astype(jnp.bfloat16)
    flattened = normed.reshape(-1, normed.shape[-1])
    hidden = jax.nn.gelu(
        jnp.dot(flattened, in_weight, preferred_element_type=jnp.float32), approximate=True
    )
    pooled = jnp.mean(hidden.reshape(local_rows, images.shape[1], -1), axis=1).astype(jnp.bfloat16)
    image_emb = jnp.dot(pooled, out_weight, preferred_element_type=jnp.float32)
    image_unit, image_len = unit_rows(image_emb)
    image_vec = image_unit.astype(jnp.bfloat16)
    scores = multiplier * lax.dot_general(
        image_vec, all_text, (((1,), (1,)), ((), ())), preferred_element_type=jnp.float32
    )
    row_high = jnp.max(scores, axis=1, keepdims=True)
    row_lse = row_high[:, 0] + jnp.log(jnp.sum(jnp.exp(scores - row_high), axis=1))
    column_ids = jnp.arange(total_rows, dtype=jnp.int32)
    target = column_ids[None, :] == pair_index[:, None]
    positive = jnp.sum(jnp.where(target, scores, jnp.zeros_like(scores)), axis=1)
    all_images = whole_of(image_vec, (("dp_0", "dp_1"), ("dp_2", "dp_3")), 0)
    all_row_lse, all_pairs = turned_gather((row_lse, pair_index.astype(jnp.float32)), DP, (0, 0))
    text_scores = multiplier * lax.dot_general(
        text_vec, all_images, (((1,), (1,)), ((), ())), preferred_element_type=jnp.float32
    )
    text_high = jnp.max(text_scores, axis=1, keepdims=True)
    col_lse_own = text_high[:, 0] + jnp.log(jnp.sum(jnp.exp(text_scores - text_high), axis=1))
    own_ids = (first_row + jnp.arange(local_rows, dtype=jnp.int32)).astype(jnp.float32)
    text_target = all_pairs[None, :] == own_ids[:, None]
    text_weights = (
        jnp.exp(text_scores - all_row_lse[None, :])
        + jnp.exp(text_scores - col_lse_own[:, None])
        - 2.0 * text_target.astype(jnp.float32)
    ).astype(jnp.bfloat16)
    grad_text_unit = multiplier * jnp.dot(
        text_weights, all_images, preferred_element_type=jnp.float32
    )
    col_lse_all = whole_of(col_lse_own, (("dp_0", "dp_1"), ("dp_2", "dp_3")), 0)
    weights = (
        jnp.exp(scores - row_lse[:, None])
        + jnp.exp(scores - col_lse_all[None, :])
        - 2.0 * target.astype(jnp.float32)
    ).astype(jnp.bfloat16)
    loss_part = jnp.sum(row_lse) + jnp.sum(col_lse_own) - 2.0 * jnp.sum(positive)
    grad_image_unit = multiplier * jnp.dot(weights, all_text, preferred_element_type=jnp.float32)
    grad_image = unit_backward(grad_image_unit, image_unit, image_len)
    grad_text = unit_backward(grad_text_unit, text_unit, text_len)
    square_part = jnp.sum(grad_image * grad_image) + jnp.sum(grad_text * grad_text)
    loss_total, squares = in_one((loss_part, square_part), (("dp_0", "dp_1"), ("dp_2", "dp_3")))
    loss = loss_total / (2.0 * total_rows)
    factor = lax.rsqrt(squares / (2.0 * total_rows * width) + 1e-06)
    return (loss.reshape(1), jnp.sqrt(squares).reshape(1), grad_image * factor, grad_text * factor)


def solution(mesh):
    torus = Mesh(mesh.devices.reshape(8, 4, 4, 2), ("dp_0", "dp_1", "dp_2", "dp_3"))
    return jax.shard_map(
        per_device,
        mesh=torus,
        in_specs=(P(DP, None, None), P(), P(), P(), P(DP, None), P(DP), P()),
        out_specs=(P(), P(), P(DP, None), P(DP, None)),
        check_vma=False,
    )
```

profile of v0, /device:TPU:1, one launch (start us, length us, event | category | flops | bytes accessed | tf_op | source)
XLA Modules:
  0.0 258.0 jit_solution(7069101414245393673)
XLA Ops:
  0.6 1.0 fusion.12
  1.6 0.8 fusion.31
  2.4 0.8 broadcast_in_dim.20
  3.2 11.9 %all-to-all-start = ((bf16[32,4,1024]{2,1,0:T(4,128)(2,1)}), bf16[32,4,1024]{2,1,0:T(4,128)(2,1)S(1)}, u32[]{:S(2)}, u32[]{:S(2)}) async-start(bf16[32,4,1024]{2,1,0:T(4,128)(2,1)} %broadcast_in_dim.20), calls=%async_computation | async-start | bytes 524288 | tf_op jit(solution)/shard_map/all_to_all | solution.py:16
  15.0 3.3 %convert_reduce_fusion = f32[4,92]{0,1:T(8,128)S(1)} fusion(bf16[4,92,4096]{2,0,1:T(4,128)(2,1)} %param.7), kind=kLoop, calls=%fused_computation.1 | loop fusion | flops 3014288 | bytes 3016128 | tf_op jit(solution)/shard_map/reduce_sum | solution.py:82
  18.3 2.1 fusion.2
  20.4 3.2 %fusion.4 = bf16[4,92,4096]{2,0,1:T(4,128)(2,1)S(1)} fusion(bf16[4,92,4096]{2,0,1:T(4,128)(2,1)S(1)} %copy-done.1, f32[4096]{0:T(1024)S(1)} %copy-done.4, f32[4,92]{0,1:T(8,128)S(1)} %add_rsqrt_fusion, f32[4,92]{0,1:T(8,128)S(1)} %broadcast_multiply_fusion), kind=kLoop, calls=%fused_computation.6 | loop fusion | flops 7536640 | bytes 6048640 | tf_op jit(solution)/shard_map/convert_element_type | solution.py:85
  23.7 3.3 %copy.27 = bf16[4,92,4096]{2,1,0:T(8,128)(2,1)} copy(bf16[4,92,4096]{2,0,1:T(4,128)(2,1)S(1)} %fusion.4) | data formatting | bytes 6029312 | tf_op jit(solution)/shard_map/convert_element_type | solution.py:85
  27.0 3.4 %reshape.128 = bf16[368,4096]{1,0:T(8,128)(2,1)} reshape(bf16[4,92,4096]{2,1,0:T(8,128)(2,1)} %copy.27) | data formatting | bytes 6029312 | tf_op jit(solution)/shard_map/reshape | solution.py:86
  30.4 9.0 %fusion.11 = f32[368,1024]{1,0:T(8,128)} fusion(bf16[368,4096]{1,0:T(8,128)(2,1)} %reshape.128, bf16[4096,1024]{1,0:T(8,128)(2,1)} %param.9), kind=kOutput, calls=%fused_computation.14 | convolution fusion | flops 3090022400 | bytes 12910592 | tf_op jit(solution)/shard_map/dot_general | solution.py:88
  39.3 2.7 %reshape.129 = f32[4,92,1024]{2,1,0:T(8,128)} reshape(f32[368,1024]{1,0:T(8,128)} %fusion.11) | data formatting | bytes 3014656 | tf_op jit(solution)/shard_map/reshape | solution.py:90
  42.0 1.5 reduce_sum.150
  43.6 0.5 multiply_reduce_fusion.4
  44.3 19.8 %all_to_all.43 = bf16[32,4,1024]{2,1,0:T(4,128)(2,1)S(1)} all-to-all(bf16[32,4,1024]{2,1,0:T(4,128)(2,1)S(1)} %broadcast_in_dim.22), channel_id=1, replica_groups=mesh['dp_0'=8,'dp_1'=4,'dp_2'=4,'dp_3'=2] {'dp_0','dp_1'}, dimensions={0} | all-to-all | bytes 524288 | tf_op jit(solution)/shard_map/all_to_all | solution.py:16
  64.1 0.7 broadcast_in_dim.21
  64.8 33.8 %all_to_all.44 = bf16[8,32,4,1024]{3,2,1,0:T(4,128)(2,1)} all-to-all(bf16[8,32,4,1024]{3,2,1,0:T(4,128)(2,1)S(1)} %broadcast_in_dim.21), channel_id=1, replica_groups=mesh['dp_0'=8,'dp_1'=4,'dp_2'=4,'dp_3'=2] {'dp_2','dp_3'}, dimensions={0} | all-to-all | bytes 4194304 | tf_op jit(solution)/shard_map/all_to_all | solution.py:16
  98.6 2.0 broadcast_in_dim.23
  100.6 5.4 %all-to-all-start.3 = ((bf16[8,32,4,1024]{3,2,1,0:T(4,128)(2,1)}), bf16[8,32,4,1024]{3,2,1,0:T(4,128)(2,1)}, u32[]{:S(2)}, u32[]{:S(2)}) async-start(bf16[8,32,4,1024]{3,2,1,0:T(4,128)(2,1)} %broadcast_in_dim.23), calls=%async_computation.3 | async-start | bytes 4194304 | tf_op jit(solution)/shard_map/all_to_all | solution.py:16
  106.7 4.1 %copy.28 = bf16[32,8,4,1024]{3,2,1,0:T(4,128)(2,1)} copy(bf16[32,8,4,1024]{3,2,0,1:T(4,128)(2,1)} %bitcast.35) | data formatting | bytes 4194304 | tf_op jit(solution)/shard_map/transpose | solution.py:30
  110.8 4.0 %reshape_reshape.6 = bf16[1024,1024]{1,0:T(8,128)(2,1)} reshape(bf16[32,8,4,1024]{3,2,1,0:T(4,128)(2,1)} %copy.28) | data formatting | bytes 4194304 | tf_op jit(solution)/shard_map/reshape;reshape | solution.py:24
  114.8 17.6 %all-to-all-done.3 = bf16[8,32,4,1024]{3,2,1,0:T(4,128)(2,1)} async-done(((bf16[8,32,4,1024]{3,2,1,0:T(4,128)(2,1)}), bf16[8,32,4,1024]{3,2,1,0:T(4,128)(2,1)}, u32[]{:S(2)}, u32[]{:S(2)}) %all-to-all-start.3) | async-done | bytes 2097184 | tf_op jit(solution)/shard_map/all_to_all | solution.py:16
  132.4 4.1 %copy.29 = bf16[32,8,4,1024]{3,2,1,0:T(4,128)(2,1)} copy(bf16[32,8,4,1024]{3,2,0,1:T(4,128)(2,1)} %bitcast.2) | data formatting | bytes 4194304 | tf_op jit(solution)/shard_map/transpose | solution.py:30
  136.4 4.0 %reshape_reshape.7 = bf16[1024,1024]{1,0:T(8,128)(2,1)} reshape(bf16[32,8,4,1024]{3,2,1,0:T(4,128)(2,1)} %copy.29) | data formatting | bytes 4194304 | tf_op jit(solution)/shard_map/reshape;reshape | solution.py:24
  140.4 2.5 fusion.38
  142.9 0.8 fusion.37
  143.7 0.2 exponential_reduce_fusion
  143.9 0.7 select_reduce_fusion
  144.6 0.6 fusion.32
  145.3 0.6 broadcast_in_dim.25
  145.9 3.8 %all-to-all-start.4 = ((f32[32,1,4]{2,1,0:T(1,128)}), f32[32,1,4]{2,1,0:T(1,128)S(1)}, u32[]{:S(2)}, u32[]{:S(2)}) async-start(f32[32,1,4]{2,1,0:T(1,128)} %broadcast_in_dim.25), calls=%async_computation.4 | async-start | bytes 32768 | tf_op jit(solution)/shard_map/all_to_all | solution.py:16
  149.7 63.0 %all-gather = f32[256,4,2]{1,2,0:T(2,128)S(1)} all-gather(f32[1,4,2]{1,2,0:T(2,128)S(1)} %maximum_bitcast_fusion), channel_id=1, replica_groups=mesh['dp_0'=8,'dp_1'=4,'dp_2'=4,'dp_3'=2] {'dp_0','dp_1','dp_2','dp_3'}, dimensions={0}, use_global_device_ids=true | all-gather | bytes 8224 | tf_op jit(solution)/shard_map/all_gather | solution.py:37
  212.7 0.2 reshape.134
  212.9 2.1 multiply_reduce_fusion.1
  215.2 0.7 reshape.135
  215.9 3.4 %all-to-all-start.5 = ((f32[8,1,128]{2,1,0:T(1,128)}), f32[8,1,128]{2,1,0:T(1,128)S(1)}, u32[]{:S(2)}, u32[]{:S(2)}) async-start(f32[8,1,128]{2,1,0:T(1,128)} %reshape.135), calls=%async_computation.5 | async-start | bytes 8192 | tf_op jit(solution)/shard_map/all_to_all | solution.py:16
  219.2 0.7 multiply_reduce_fusion
  221.8 1.9 all-to-all-done.5
  223.8 0.5 broadcast.82
  224.3 0.7 reduce.3
  225.0 0.1 copy.31
  225.2 0.1 sub.84
  225.3 2.1 multiply_reduce_fusion.3
  227.4 0.7 multiply_reduce_fusion.2
  229.5 7.6 %all_to_all.45 = f32[8,1,2]{2,1,0:T(1,128)S(1)} all-to-all(f32[8,1,2]{2,1,0:T(1,128)S(1)} %broadcast_in_dim.28), channel_id=1, replica_groups=mesh['dp_0'=8,'dp_1'=4,'dp_2'=4,'dp_3'=2] {'dp_2','dp_3'}, dimensions={0} | all-to-all | bytes 128 | tf_op jit(solution)/shard_map/all_to_all | solution.py:16
  237.2 14.6 %all_to_all.46 = f32[32,1,2]{2,1,0:T(1,128)S(1)} all-to-all(f32[32,1,2]{2,1,0:T(1,128)S(1)} %broadcast_in_dim.29), channel_id=1, replica_groups=mesh['dp_0'=8,'dp_1'=4,'dp_2'=4,'dp_3'=2] {'dp_0','dp_1'}, dimensions={0} | all-to-all | bytes 512 | tf_op jit(solution)/shard_map/all_to_all | solution.py:16
  251.8 0.6 fusion.36
  253.8 0.6 broadcast_multiply_fusion.2
  254.4 0.6 broadcast_multiply_fusion.1
  (34 shorter events, 0.6 us)
Async XLA Ops:
  0.6 42.9 %copy-start = (bf16[1024,1024]{1,0:T(8,128)(2,1)S(1)}, bf16[1024,1024]{1,0:T(8,128)(2,1)}, u32[]{:S(2)}) copy-start(bf16[1024,1024]{1,0:T(8,128)(2,1)} %param.10) | copy-start | bytes 6291460
  3.2 41.0 %all-to-all-start = ((bf16[32,4,1024]{2,1,0:T(4,128)(2,1)}), bf16[32,4,1024]{2,1,0:T(4,128)(2,1)S(1)}, u32[]{:S(2)}, u32[]{:S(2)}) async-start(bf16[32,4,1024]{2,1,0:T(4,128)(2,1)} %broadcast_in_dim.20), calls=%async_computation | async-start | bytes 524288 | tf_op jit(solution)/shard_map/all_to_all | solution.py:16
  15.0 3.3 %copy-start.1 = (bf16[4,92,4096]{2,0,1:T(4,128)(2,1)S(1)}, bf16[4,92,4096]{2,0,1:T(4,128)(2,1)}, u32[]{:S(2)}) copy-start(bf16[4,92,4096]{2,0,1:T(4,128)(2,1)} %param.7) | copy-start | bytes 9043972
  18.3 2.1 copy-start.4
  100.6 6.1 %copy-start.5 = (s32[4]{0:T(128)S(1)}, s32[4]{0:T(128)}, u32[]{:S(2)}) copy-start(s32[4]{0:T(128)} %param.12) | copy-start | bytes 52
  100.6 31.8 %all-to-all-start.3 = ((bf16[8,32,4,1024]{3,2,1,0:T(4,128)(2,1)}), bf16[8,32,4,1024]{3,2,1,0:T(4,128)(2,1)}, u32[]{:S(2)}, u32[]{:S(2)}) async-start(bf16[8,32,4,1024]{3,2,1,0:T(4,128)(2,1)} %broadcast_in_dim.23), calls=%async_computation.3 | async-start | bytes 4194304 | tf_op jit(solution)/shard_map/all_to_all | solution.py:16
  140.4 2.5 copy-start.2
  142.9 70.0 %copy-start.3 = (bf16[4,1024]{1,0:T(4,128)(2,1)S(1)}, bf16[4,1024]{1,0:T(4,128)(2,1)}, u32[]{:S(2)}) copy-start(bf16[4,1024]{1,0:T(4,128)(2,1)} %param.11) | copy-start | bytes 24580
  145.9 69.2 %all-to-all-start.4 = ((f32[32,1,4]{2,1,0:T(1,128)}), f32[32,1,4]{2,1,0:T(1,128)S(1)}, u32[]{:S(2)}, u32[]{:S(2)}) async-start(f32[32,1,4]{2,1,0:T(1,128)} %broadcast_in_dim.25), calls=%async_computation.4 | async-start | bytes 32768 | tf_op jit(solution)/shard_map/all_to_all | solution.py:16
  215.9 7.9 %all-to-all-start.5 = ((f32[8,1,128]{2,1,0:T(1,128)}), f32[8,1,128]{2,1,0:T(1,128)S(1)}, u32[]{:S(2)}, u32[]{:S(2)}) async-start(f32[8,1,128]{2,1,0:T(1,128)} %reshape.135), calls=%async_computation.5 | async-start | bytes 8192 | tf_op jit(solution)/shard_map/all_to_all | solution.py:16
where the time goes:
time: 259 us; the launch traced here: 258 us
  blocking collectives  139 us (54%)
  local copies, waits for them, and re-layouts  32.1 us (12%)
  starting transfers between devices  24.5 us (9%)
  waiting for transfers between devices  19.6 us (8%)
  other arithmetic  17 us (7%)
  matrix products  17 us (7%)
  between operations  9.03 us (3%)
    all_to_all x4, blocking collectives, from_everyone(): lax.all_to_all(jnp.broadcast_to(array[None], (size, *array.shape)), axis,...  75.8 us
    all_gather x1, blocking collectives, turned_gather(): lax.all_gather(both, axis, axis=0, tiled=True)  63 us
    all_to_all x4, starting transfers between devices, from_everyone(): lax.all_to_all(jnp.broadcast_to(array[None], (size, *array.shape)), axis,...  24.5 us
    all_to_all x4, waiting for transfers between devices, from_everyone(): lax.all_to_all(jnp.broadcast_to(array[None], (size, *array.shape)), axis,...  19.6 us
    dot_general x1, matrix products, per_device(): jnp.dot(flattened, in_weight, preferred_element_type=jnp.float32)  8.96 us
    transpose x4, local copies, waits for them, and re-layouts, whole_of(): blocks = jnp.swapaxes(from_everyone(first, near), 0, 1)  8.27 us
    another operation x2, local copies, waits for them, and re-layouts, laid_out(): return jnp.moveaxis(blocks, 0, dim).reshape(lengths)  7.93 us
  transfers between devices with their start and end apart: 4, of which 2 were waited for; matrix products, arithmetic and copies ran while one was open for 16% of the time, Pallas kernels for 0%

commit v1 on v0

v1 whole, which is shorter than its diff:
```python
import functools

import jax
import jax.numpy as jnp
from jax import lax
from jax.experimental import pallas as pl
from jax.experimental.pallas import tpu as pltpu
from jax.sharding import Mesh
from jax.sharding import PartitionSpec as P

AXES = ("z", "x", "y", "c")
NZ, NX, NY = 8, 4, 4
EPS_UNIT = 1e-06
EPS_LAYER = 1e-05
F32 = jnp.float32
BF16 = jnp.bfloat16
TOKENS, WIDE, E, HALF, ROWS = 92, 4096, 1024, 512, 1024
PAD = 96


def coordinates():
    return tuple(lax.axis_index(a) for a in AXES)


def remote(src, dst, send_sem, recv_sem, where):
    return pltpu.make_async_remote_copy(
        src_ref=src,
        dst_ref=dst,
        send_sem=send_sem,
        recv_sem=recv_sem,
        device_id=where,
        device_id_type=pl.DeviceIdType.MESH,
    )


Z_ORDER = (4, 3, 5, 2, 6, 1, 7, 0)
RING = (2, 1, 3)


class Gather:
    def __init__(self, place, send, line, whole, sems):
        self.z, self.x, self.y, self.c = place
        self.send, self.line, self.whole = send, line, whole
        (self.s1, self.r1, self.s2, self.r2, self.s3, self.r3, self.s4, self.r4) = sems
        self.copies = []
        self.second = {}
        self.third = {}
        self.cross = {}

    def block(self, q, p):
        c = self.c
        x = lax.rem(self.x + NX - q * (1 - c) + NX - p * c, NX)
        y = lax.rem(self.y + NY - q * c + NY - p * (1 - c), NY)
        return x * NY + y

    def start_line(self):
        j = self.c * NZ + self.z
        self.first = []
        for oz in Z_ORDER:
            for oc in range(2):
                if oz == 0 and oc == 0:
                    continue
                tz, tc = lax.rem(self.z + oz, NZ), lax.rem(self.c + oc, 2)
                o = oz * 2 + oc
                copy = remote(
                    self.send.at[tc], self.line.at[j], self.s1.at[o], self.r1.at[o], (tz, self.x, self.y, tc)
                )
                copy.start()
                self.first.append(copy)
        self.line[j] = self.send[self.c]
        self.copies += self.first

    def finish_line(self):
        for copy in self.first:
            copy.wait_recv()
        c, b = self.c, self.block(0, 0)
        for j in range(2 * NZ):
            r = (j % NZ) * 4
            self.whole[c, j // NZ, b, r : r + 4, :] = self.line[j]

    def start_second(self):
        c, b = self.c, self.block(0, 0)
        here = self.whole.at[c, :, b]
        for o in RING:
            where = (self.z, lax.rem(self.x + o * (1 - c), NX), lax.rem(self.y + o * c, NY), c)
            copy = remote(here, here, self.s2.at[o], self.r2.at[o], where)
            copy.start()
            self.second[o] = copy
            self.copies.append(copy)
        self.forward(0)

    def to_partner(self, q, p):
        here = self.whole.at[self.c, :, self.block(q, p)]
        copy = remote(here, here, self.s4.at[q * 4 + p], self.r4.at[q * 4 + p], (self.z, self.x, self.y, 1 - self.c))
        copy.start()
        self.cross[q, p] = copy
        self.copies.append(copy)

    def forward(self, q):
        c = self.c
        here = self.whole.at[c, :, self.block(q, 0)]
        for p in RING:
            where = (self.z, lax.rem(self.x + p * c, NX), lax.rem(self.y + p * (1 - c), NY), c)
            copy = remote(here, here, self.s3.at[q * 4 + p], self.r3.at[q * 4 + p], where)
            copy.start()
            self.third[q, p] = copy
            self.copies.append(copy)
        self.to_partner(q, 0)

    def finish_second(self):
        for o in (1, 3, 2):
            self.second[o].wait_recv()
            self.forward(o)

    def finish_third(self):
        for q in (0, 1, 3, 2):
            for p in (1, 3, 2):
                self.third[q, p].wait_recv()
                self.to_partner(q, p)

    def finish_cross(self):
        for q in (0, 1, 3, 2):
            for p in (0, 1, 3, 2):
                self.cross[q, p].wait_recv()

    def drain(self):
        for copy in self.copies:
            copy.wait_send()


class SmallGather:
    def __init__(self, place, send, line, whole, sems):
        self.z, self.x, self.y, self.c = place
        self.send, self.line, self.whole = send, line, whole
        (self.s1, self.r1, self.s2, self.r2, self.s3, self.r3) = sems
        self.copies = []
        self.second = {}
        self.third = {}

    block = Gather.block

    def start_line(self):
        j = self.c * NZ + self.z
        self.first = []
        for oz in Z_ORDER:
            for oc in range(2):
                if oz == 0 and oc == 0:
                    continue
                tz, tc = lax.rem(self.z + oz, NZ), lax.rem(self.c + oc, 2)
                o = oz * 2 + oc
                copy = remote(self.send, self.line.at[j], self.s1.at[o], self.r1.at[o], (tz, self.x, self.y, tc))
                copy.start()
                self.first.append(copy)
        self.line[j] = self.send[...]
        self.copies += self.first

    def finish_line(self):
        for copy in self.first:
            copy.wait_recv()
        total = self.line[0]
        for j in range(1, 2 * NZ):
            total = total + self.line[j]
        self.whole[self.block(0, 0)] = total

    def start_second(self):
        c = self.c
        here = self.whole.at[self.block(0, 0)]
        for o in RING:
            where = (self.z, lax.rem(self.x + o * (1 - c), NX), lax.rem(self.y + o * c, NY), c)
            copy = remote(here, here, self.s2.at[o], self.r2.at[o], where)
            copy.start()
            self.second[o] = copy
            self.copies.append(copy)
        self.forward(0)

    def forward(self, q):
        c = self.c
        here = self.whole.at[self.block(q, 0)]
        for p in RING:
            where = (self.z, lax.rem(self.x + p * c, NX), lax.rem(self.y + p * (1 - c), NY), c)
            copy = remote(here, here, self.s3.at[q * 4 + p], self.r3.at[q * 4 + p], where)
            copy.start()
            self.third[q, p] = copy
            self.copies.append(copy)

    def finish_second(self):
        for o in (1, 3, 2):
            self.second[o].wait_recv()
            self.forward(o)

    def finish_third(self):
        for q in (0, 1, 3, 2):
            for p in (1, 3, 2):
                self.third[q, p].wait_recv()

    drain = Gather.drain


def spread(values, first_lane):
    lanes = lax.broadcasted_iota(jnp.int32, (4, 128), 1) - lax.broadcasted_iota(jnp.int32, (4, 128), 0)
    return jnp.sum(jnp.where(lanes == first_lane, values, 0.0), axis=0, keepdims=True)


def unit_rows(matrix):
    length = jnp.sqrt(jnp.sum(matrix * matrix, axis=1, keepdims=True) + EPS_UNIT)
    return matrix / length, length


def columns_of(whole, out, kinds):
    eye = lax.broadcasted_iota(jnp.int32, (128, 128), 0) == lax.broadcasted_iota(jnp.int32, (128, 128), 1)
    for b in range(NX * NY):
        column = jnp.sum(jnp.where(eye, jnp.broadcast_to(whole[b], (128, 128)), 0.0), axis=1, keepdims=True)
        for k in range(kinds):
            out[k, b * 32 : b * 32 + 32, :] = column[k * 32 : k * 32 + 32]


def kernel(
    images, gain, in_weight, out_weight, text, pair, scale,
    loss, norm, update_image, update_text,
    pixels, normed, w, ow, pooled,
    text_send, text_line, text_all, image_send, image_line, image_all,
    tag_send, tag_line, tag_all, len_send, len_line, len_all,
    scores, weights, row_lse, tags, lens, grad, own, swap_out, swap_in,
    load_sem, swap_sem, *sems,
):
    place = coordinates()
    z, x, y, c = place
    text_gather = Gather(place, text_send, text_line, text_all, sems[0:8])
    image_gather = Gather(place, image_send, image_line, image_all, sems[8:16])
    tag_gather = SmallGather(place, tag_send, tag_line, tag_all, sems[16:22])
    len_gather = SmallGather(place, len_send, len_line, len_all, sems[22:28])

    loads = []
    for i in range(4):
        loads.append(pltpu.make_async_copy(images.at[i], pixels.at[i], load_sem.at[i]))
    for n in range(4):
        part = pl.ds(n * 256, 256)
        loads.append(pltpu.make_async_copy(in_weight.at[:, part], w.at[n], load_sem.at[4 + n]))
    loads.append(pltpu.make_async_copy(out_weight, ow, load_sem.at[8]))
    for copy in loads:
        copy.start()

    barrier = pltpu.get_barrier_semaphore()
    peers = []
    for oz in range(NZ):
        for oc in range(2):
            if oz or oc:
                peers.append((lax.rem(z + oz, NZ), x, y, lax.rem(c + oc, 2)))
    for o in (1, 2, 3):
        peers.append((z, lax.rem(x + o, NX), y, c))
        peers.append((z, x, lax.rem(y + o, NY), c))
    for where in peers:
        pl.semaphore_signal(barrier, inc=1, device_id=where, device_id_type=pl.DeviceIdType.MESH)

    text_unit, text_len = unit_rows(text[...].astype(F32))
    text_vec = text_unit.astype(BF16)
    for k in range(2):
        text_send[k] = text_vec[:, k * HALF : (k + 1) * HALF]
    lane = lax.broadcasted_iota(jnp.int32, (1, 128), 1)
    first_lane = (c * NZ + z) * 4
    tag = spread(text_len, first_lane + 64)
    for i in range(4):
        t = pair[i]
        row = (((t >> 2) & 1) << 9) | (((t >> 5) & 3) << 7) | (((t >> 3) & 3) << 5) | ((t >> 7) << 2) | (t & 3)
        tag = tag + jnp.where(lane == first_lane + i, row.astype(F32), 0.0)
    tag_send[...] = tag

    pl.semaphore_wait(barrier, len(peers))
    text_gather.start_line()
    tag_gather.start_line()

    def normalise(i, carry):
        for start in range(0, TOKENS, 32):
            size = min(32, TOKENS - start)
            rows = pl.ds(start, size)
            total = jnp.zeros((size, 128), F32)
            for k in range(WIDE // 128):
                total = total + pixels[i, rows, k * 128 : (k + 1) * 128].astype(F32)
            average = jnp.sum(total, axis=1, keepdims=True) * (1.0 / WIDE)
            total = jnp.zeros((size, 128), F32)
            for k in range(WIDE // 128):
                centered = pixels[i, rows, k * 128 : (k + 1) * 128].astype(F32) - average
                total = total + centered * centered
            variance = jnp.sum(total, axis=1, keepdims=True) * (1.0 / WIDE)
            factor = lax.rsqrt(variance + EPS_LAYER)
            for k in range(WIDE // 128):
                part = slice(k * 128, (k + 1) * 128)
                centered = pixels[i, rows, part].astype(F32) - average
                normed[i, rows, part] = (centered * factor * gain[:, part]).astype(BF16)
        return carry

    for i in range(4):
        loads[i].wait()
    normed[:, 80:PAD, :] = jnp.zeros((4, 16, WIDE), BF16)
    lax.fori_loop(0, 4, normalise, 0)

    text_gather.finish_line()
    tag_gather.finish_line()
    text_gather.start_second()
    tag_gather.start_second()

    pooled[...] = jnp.zeros_like(pooled)
    for n in range(4):
        loads[4 + n].wait()

    def encode(n, carry):
        flat = normed[...].reshape(4 * PAD, WIDE)
        hidden = jax.nn.gelu(jnp.dot(flat, w[n], preferred_element_type=F32), approximate=True)
        for i in range(4):
            mean = jnp.sum(hidden[i * PAD : i * PAD + TOKENS], axis=0, keepdims=True) * (1.0 / TOKENS)
            pooled[n, i : i + 1, :] = mean
        return carry

    lax.fori_loop(0, 2, encode, 0)
    text_gather.finish_second()
    tag_gather.finish_second()
    lax.fori_loop(2, 4, encode, 0)
    loads[8].wait()
    image_emb = jnp.zeros((8, E), F32)
    for n in range(4):
        image_emb = image_emb + jnp.dot(
            pooled[n].astype(BF16), ow[n * 256 : (n + 1) * 256, :], preferred_element_type=F32
        )
    image_unit, image_len = unit_rows(image_emb[0:4])
    image_vec = image_unit.astype(BF16)
    for k in range(2):
        image_send[k] = image_vec[:, k * HALF : (k + 1) * HALF]
    len_send[...] = spread(image_len, first_lane)
    image_gather.start_line()
    len_gather.start_line()

    text_gather.finish_third()
    tag_gather.finish_third()
    columns_of(tag_all, tags, 4)
    image_gather.finish_line()
    len_gather.finish_line()
    image_gather.start_second()
    len_gather.start_second()
    text_gather.finish_cross()
    image_gather.finish_second()
    len_gather.finish_second()
    image_gather.finish_third()
    len_gather.finish_third()
    image_gather.finish_cross()
    columns_of(len_all, lens, 2)

    multiplier = scale[0]

    def score(chunk, carry):
        side, b = chunk // 2, (chunk % 2) * 8
        total = jnp.zeros((256, ROWS), F32)
        for k in range(2):
            total = total + lax.dot_general(
                image_all[k, side, pl.ds(b, 8)].reshape(256, HALF),
                text_all[k].reshape(ROWS, HALF),
                (((1,), (1,)), ((), ())),
                preferred_element_type=F32,
            )
        scores[pl.ds(pl.multiple_of(chunk * 256, 256), 256), :] = total * multiplier
        return carry

    lax.fori_loop(0, 4, score, 0)

    def over_rows(r, high):
        rows = pl.ds(pl.multiple_of(r * 32, 32), 32)
        s = scores[rows, :]
        top = jnp.max(s, axis=1, keepdims=True)
        row_lse[rows, :] = top + jnp.log(jnp.sum(jnp.exp(s - top), axis=1, keepdims=True))
        return jnp.maximum(high, jnp.max(s.reshape(4, 8, ROWS), axis=0))

    high = lax.fori_loop(0, 32, over_rows, jnp.full((8, ROWS), -jnp.inf, F32))
    high = jnp.max(high, axis=0, keepdims=True)

    def over_columns(r, total):
        rows = pl.ds(pl.multiple_of(r * 32, 32), 32)
        return total + jnp.sum(jnp.exp(scores[rows, :] - high).reshape(4, 8, ROWS), axis=0)

    total = lax.fori_loop(0, 32, over_columns, jnp.zeros((8, ROWS), F32))
    col_lse = high + jnp.log(jnp.sum(total, axis=0, keepdims=True))

    ids = lax.broadcasted_iota(jnp.int32, (32, ROWS), 1).astype(F32)

    def weigh(r, positive):
        rows = pl.ds(pl.multiple_of(r * 32, 32), 32)
        s = scores[rows, :]
        hit = ids == tags[r // 16, pl.ds(pl.multiple_of((r % 16) * 32, 32), 32), :]
        value = jnp.exp(s - row_lse[rows, :]) + jnp.exp(s - col_lse) - jnp.where(hit, 2.0, 0.0)
        weights[r // 16, pl.ds(pl.multiple_of((r % 16) * 32, 32), 32), :] = value.astype(BF16)
        return positive + jnp.sum(jnp.where(hit, s, 0.0).reshape(4, 8, ROWS), axis=0)

    positive = lax.fori_loop(0, 32, weigh, jnp.zeros((8, ROWS), F32))
    loss[0] = (jnp.sum(row_lse[...]) + jnp.sum(col_lse) - 2.0 * jnp.sum(positive)) * (0.5 / ROWS)

    squares = jnp.zeros((HALF, 1), F32)
    b = x * NY + y
    for side in range(2):
        vectors = image_all if side == 0 else text_all
        others = text_all if side == 0 else image_all
        size = jnp.zeros((HALF, 1), F32)
        along = jnp.zeros((HALF, 1), F32)
        for k in range(2):
            if side == 0:
                left = weights[c]
                g = jnp.dot(left, others[k].reshape(ROWS, HALF), preferred_element_type=F32)
            else:
                left = weights[:, :, pl.ds(pl.multiple_of(c * HALF, HALF), HALF)].reshape(ROWS, HALF)
                g = lax.dot_general(
                    left, others[k].reshape(ROWS, HALF), (((0,), (0,)), ((), ())), preferred_element_type=F32
                )
            g = g * multiplier
            grad[...] = g.reshape(NX * NY, 32, HALF)
            mine = grad[b].reshape(8, 4, HALF)
            which = lax.broadcasted_iota(jnp.int32, (8, 4, HALF), 0) == z
            own[side, :, k * HALF : (k + 1) * HALF] = jnp.sum(jnp.where(which, mine, 0.0), axis=0)
            u = vectors[k, c].reshape(HALF, HALF).astype(F32)
            size = size + jnp.sum(g * g, axis=1, keepdims=True)
            along = along + jnp.sum(g * u, axis=1, keepdims=True)
        length = lens[c] if side == 0 else tags[2 + c]
        inverse = 1.0 / (length * length)
        squares = squares + (size - along * along * (1.0 + EPS_UNIT * inverse)) * inverse

    swap_out[...] = jnp.broadcast_to(jnp.sum(squares, axis=0, keepdims=True), (8, 128))
    swap = remote(swap_out, swap_in, swap_sem.at[0], swap_sem.at[1], (z, x, y, 1 - c))
    swap.start()

    def own_gradient(g, unit, length):
        return (g - unit * jnp.sum(unit * g, axis=1, keepdims=True)) / length

    grad_image = own_gradient(own[0], image_unit, image_len)
    grad_text = own_gradient(own[1], text_unit, text_len)
    swap.wait_recv()
    total = swap_out[...] + swap_in[...]
    factor = lax.rsqrt(total[0:1, 0:1] * (1.0 / (2.0 * ROWS * E)) + 1e-06)
    update_image[...] = grad_image * factor
    update_text[...] = grad_text * factor
    norm[0] = jnp.sqrt(jnp.sum(total) * (1.0 / (8.0 * 128.0)))
    swap.wait_send()
    for gather in (text_gather, tag_gather, image_gather, len_gather):
        gather.drain()


def per_device(images, layer_gain, in_weight, out_weight, text_embed, pair_index, logit_scale):
    any_space = pl.BlockSpec(memory_space=pl.ANY)
    vmem = pl.BlockSpec(memory_space=pltpu.VMEM)
    smem = pl.BlockSpec(memory_space=pltpu.SMEM)
    dma = pltpu.SemaphoreType.DMA
    big = [dma((16,)), dma((16,)), dma((4,)), dma((4,)), dma((16,)), dma((16,)), dma((16,)), dma((16,))]
    small = big[:6]
    matrix = [
        pltpu.VMEM((2, 4, HALF), BF16),
        pltpu.VMEM((2 * NZ, 4, HALF), BF16),
        pltpu.VMEM((2, 2, NX * NY, 32, HALF), BF16),
    ]
    lanes = [pltpu.VMEM((1, 128), F32), pltpu.VMEM((2 * NZ, 1, 128), F32), pltpu.VMEM((NX * NY, 1, 128), F32)]
    return pl.pallas_call(
        kernel,
        out_shape=(
            jax.ShapeDtypeStruct((1,), F32),
            jax.ShapeDtypeStruct((1,), F32),
            jax.ShapeDtypeStruct((4, E), F32),
            jax.ShapeDtypeStruct((4, E), F32),
        ),
        in_specs=[any_space, vmem, any_space, any_space, vmem, smem, smem],
        out_specs=(smem, smem, vmem, vmem),
        scratch_shapes=[
            pltpu.VMEM((4, TOKENS, WIDE), BF16),
            pltpu.VMEM((4, PAD, WIDE), BF16),
            pltpu.VMEM((4, WIDE, 256), BF16),
            pltpu.VMEM((E, E), BF16),
            pltpu.VMEM((4, 8, 256), F32),
            *matrix,
            *matrix,
            *lanes,
            *lanes,
            pltpu.VMEM((ROWS, ROWS), F32),
            pltpu.VMEM((2, HALF, ROWS), BF16),
            pltpu.VMEM((ROWS, 1), F32),
            pltpu.VMEM((4, HALF, 1), F32),
            pltpu.VMEM((2, HALF, 1), F32),
            pltpu.VMEM((NX * NY, 32, HALF), F32),
            pltpu.VMEM((2, 4, E), F32),
            pltpu.VMEM((8, 128), F32),
            pltpu.VMEM((8, 128), F32),
            dma((9,)),
            dma((2,)),
            *big,
            *big,
            *small,
            *small,
        ],
        compiler_params=pltpu.CompilerParams(
            collective_id=0, has_side_effects=True, vmem_limit_bytes=63 * 1024 * 1024
        ),
        name="contrastive",
    )(images, layer_gain.reshape(1, WIDE), in_weight, out_weight, text_embed, pair_index, logit_scale)


def solution(mesh):
    torus = Mesh(mesh.devices.reshape(NZ, NX, NY, 2), AXES)
    return jax.shard_map(
        per_device,
        mesh=torus,
        in_specs=(P(AXES, None, None), P(), P(), P(), P(AXES, None), P(AXES), P()),
        out_specs=(P(), P(), P(AXES, None), P(AXES, None)),
        check_vma=False,
    )
```

time: 259 us -> 78.4 us (0.30)
  blocking collectives: 139 us -> 0 us
  Pallas kernels: 0 us -> 65.5 us
  starting transfers between devices: 24.5 us -> 0 us
  local copies, waits for them, and re-layouts: 32.1 us -> 7.82 us
  waiting for transfers between devices: 19.6 us -> 0 us
  matrix products: 17 us -> 0 us
  other arithmetic: 17 us -> 0 us
  between operations: 9.03 us -> 4.66 us
    all_to_all x4 -> x0, blocking collectives: 75.8 us -> none  [from_everyone(): lax.all_to_all(jnp.broadcast_to(array[None], (size, *array.shape)), axis,...]
    pallas_call x0 -> x1, Pallas kernels: none -> 65.5 us  [per_device(): pl.pallas_call(kernel, out_shape=(jax.ShapeDtypeStruct((1,), F32), jax.Sh...]
    all_gather x1 -> x0, blocking collectives: 63 us -> none  [turned_gather(): lax.all_gather(both, axis, axis=0, tiled=True)]
    all_to_all x4 -> x0, starting transfers between devices: 24.5 us -> none  [from_everyone(): lax.all_to_all(jnp.broadcast_to(array[None], (size, *array.shape)), axis,...]
    all_to_all x4 -> x0, waiting for transfers between devices: 19.6 us -> none  [from_everyone(): lax.all_to_all(jnp.broadcast_to(array[None], (size, *array.shape)), axis,...]
    dot_general x6 -> x0, matrix products: 17 us -> none  [the longest x1 8.96 us: per_device(): jnp.dot(flattened, in_weight, preferred_element_type=jnp.float32)]
    reduce_sum x11 -> x0, other arithmetic: 10.9 us -> none  [the longest x1 3.25 us: per_device(): average = jnp.mean(values, axis=-1, keepdims=True)]
    transpose x4 -> x0, local copies, waits for them, and re-layouts: 8.27 us -> none  [whole_of(): blocks = jnp.swapaxes(from_everyone(first, near), 0, 1)]
  transfers between devices with their start and end apart: 4 -> 0, of which waited for: 2 -> 0; matrix products, arithmetic and copies ran while one was open for 16% -> 0% of each run, Pallas kernels for 0% -> 0%
where the time goes in v1:
time: 78.4 us; the launch traced here: 78 us
  Pallas kernels  65.5 us (84%)
  local copies, waits for them, and re-layouts  7.82 us (10%)
  between operations  4.66 us (6%)
    pallas_call x1, Pallas kernels, per_device(): pl.pallas_call(kernel, out_shape=(jax.ShapeDtypeStruct((1,), F32), jax.Sh...  65.5 us
    unnamed x3, local copies, waits for them, and re-layouts  7.82 us

profile of v1, /device:TPU:1, one launch (start us, length us, event | category | flops | bytes accessed | tf_op | source)
XLA Modules:
  0.0 78.0 jit_solution(1414277353946960995)
XLA Ops:
  1.3 5.2 %copy.11.images = bf16[4,92,4096]{2,1,0:T(8,128)(2,1)} copy(bf16[4,92,4096]{2,0,1:T(4,128)(2,1)} %param.7) | data formatting | bytes 6029312 | tf_op args[0]
  6.5 65.5 %contrastive.1 = (f32[1]{0:T(128)}, f32[1]{0:T(128)}, f32[4,1024]{1,0:T(4,128)}, f32[4,1024]{1,0:T(4,128)}) custom-call(bf16[4,92,4096]{2,1,0:T(8,128)(2,1)} %copy.11.images, f32[1,4096]{1,0:T(1,128)} %bitcast.1, bf16[4096,1024]{1,0:T(8,128)(2,1)} %in_weight.1, bf16[1024,1024]{1,0:T(8,128)(2,1)} %out_weight.1, bf16[4,1024]{1,0:T(4,128)(2,1)} %text.1, ...), custom_call_target="tpu_custom_call" | custom-call | tf_op jit(solution)/shard_map/contrastive/pallas_call | solution.py:455
  73.1 1.3 %copy.19 = f32[4,1024]{1,0:T(4,128)} copy(f32[4,1024]{1,0:T(4,128)} %get-tuple-element.10) | data formatting | bytes 32768
  74.4 1.3 %copy.20 = f32[4,1024]{1,0:T(4,128)} copy(f32[4,1024]{1,0:T(4,128)} %get-tuple-element.11) | data formatting | bytes 32768

commit v2 on v1

--- a/solution.py
+++ b/solution.py
@@ -1,5 +1,3 @@
-import functools
-
 import jax
 import jax.numpy as jnp
 from jax import lax
@@ -15,7 +13,7 @@
 F32 = jnp.float32
 BF16 = jnp.bfloat16
 TOKENS, WIDE, E, HALF, ROWS = 92, 4096, 1024, 512, 1024
-PAD = 96
+BLOCKS = 23
 
 
 def coordinates():
@@ -232,7 +230,7 @@
 
     loads = []
     for i in range(4):
-        loads.append(pltpu.make_async_copy(images.at[i], pixels.at[i], load_sem.at[i]))
+        loads.append(pltpu.make_async_copy(images.at[:, i], pixels.at[:, :, pl.ds(4 * i, 4)], load_sem.at[i]))
     for n in range(4):
         part = pl.ds(n * 256, 256)
         loads.append(pltpu.make_async_copy(in_weight.at[:, part], w.at[n], load_sem.at[4 + n]))
@@ -270,29 +268,27 @@
     tag_gather.start_line()
 
     def normalise(i, carry):
-        for start in range(0, TOKENS, 32):
-            size = min(32, TOKENS - start)
-            rows = pl.ds(start, size)
-            total = jnp.zeros((size, 128), F32)
-            for k in range(WIDE // 128):
-                total = total + pixels[i, rows, k * 128 : (k + 1) * 128].astype(F32)
-            average = jnp.sum(total, axis=1, keepdims=True) * (1.0 / WIDE)
-            total = jnp.zeros((size, 128), F32)
-            for k in range(WIDE // 128):
-                centered = pixels[i, rows, k * 128 : (k + 1) * 128].astype(F32) - average
-                total = total + centered * centered
-            variance = jnp.sum(total, axis=1, keepdims=True) * (1.0 / WIDE)
-            factor = lax.rsqrt(variance + EPS_LAYER)
-            for k in range(WIDE // 128):
-                part = slice(k * 128, (k + 1) * 128)
-                centered = pixels[i, rows, part].astype(F32) - average
-                normed[i, rows, part] = (centered * factor * gain[:, part]).astype(BF16)
+        def tile(k):
+            return pixels[i, k].astype(F32)
+
+        total = jnp.zeros((16, 128), F32)
+        for k in range(WIDE // 128):
+            total = total + tile(k)
+        average = jnp.sum(total, axis=1, keepdims=True) * (1.0 / WIDE)
+        total = jnp.zeros((16, 128), F32)
+        for k in range(WIDE // 128):
+            centered = tile(k) - average
+            total = total + centered * centered
+        variance = jnp.sum(total, axis=1, keepdims=True) * (1.0 / WIDE)
+        factor = lax.rsqrt(variance + EPS_LAYER)
+        for k in range(WIDE // 128):
+            part = slice(k * 128, (k + 1) * 128)
+            normed[i, :, part] = ((tile(k) - average) * factor * gain[:, part]).astype(BF16)
         return carry
 
     for i in range(4):
         loads[i].wait()
-    normed[:, 80:PAD, :] = jnp.zeros((4, 16, WIDE), BF16)
-    lax.fori_loop(0, 4, normalise, 0)
+    lax.fori_loop(0, BLOCKS, normalise, 0)
 
     text_gather.finish_line()
     tag_gather.finish_line()
@@ -304,11 +300,10 @@
         loads[4 + n].wait()
 
     def encode(n, carry):
-        flat = normed[...].reshape(4 * PAD, WIDE)
+        flat = normed[...].reshape(BLOCKS * 16, WIDE)
         hidden = jax.nn.gelu(jnp.dot(flat, w[n], preferred_element_type=F32), approximate=True)
-        for i in range(4):
-            mean = jnp.sum(hidden[i * PAD : i * PAD + TOKENS], axis=0, keepdims=True) * (1.0 / TOKENS)
-            pooled[n, i : i + 1, :] = mean
+        pairs = jnp.sum(hidden.reshape(BLOCKS * 2, 8, 256), axis=0)
+        pooled[n, 0:4, :] = (pairs[0:4] + pairs[4:8]) * (1.0 / TOKENS)
         return carry
 
     lax.fori_loop(0, 2, encode, 0)
@@ -463,8 +458,8 @@
         in_specs=[any_space, vmem, any_space, any_space, vmem, smem, smem],
         out_specs=(smem, smem, vmem, vmem),
         scratch_shapes=[
-            pltpu.VMEM((4, TOKENS, WIDE), BF16),
-            pltpu.VMEM((4, PAD, WIDE), BF16),
+            pltpu.VMEM((BLOCKS, WIDE // 128, 16, 128), BF16),
+            pltpu.VMEM((BLOCKS, 16, WIDE), BF16),
             pltpu.VMEM((4, WIDE, 256), BF16),
             pltpu.VMEM((E, E), BF16),
             pltpu.VMEM((4, 8, 256), F32),
@@ -492,7 +487,7 @@
             collective_id=0, has_side_effects=True, vmem_limit_bytes=63 * 1024 * 1024
         ),
         name="contrastive",
-    )(images, layer_gain.reshape(1, WIDE), in_weight, out_weight, text_embed, pair_index, logit_scale)
+    )(images.reshape(4, BLOCKS, 4, WIDE // 128, 128).transpose(1, 2, 3, 0, 4), layer_gain.reshape(1, WIDE), in_weight, out_weight, text_embed, pair_index, logit_scale)
 
 
 def solution(mesh):

time: 78.4 us -> 74.3 us (0.948)
  local copies, waits for them, and re-layouts: 7.82 us -> 2.65 us
  Pallas kernels: 65.5 us -> 66.5 us
    unnamed x3 -> x2, local copies, waits for them, and re-layouts: 7.82 us -> 2.65 us
    pallas_call x1, Pallas kernels: 65.5 us -> 66.5 us  [per_device(): pl.pallas_call(kernel, out_shape=(jax.ShapeDtypeStruct((1,), F32), jax.Sh...]
where the time goes in v2:
time: 74.3 us; the launch traced here: 73.9 us
  Pallas kernels  66.5 us (90%)
  between operations  4.78 us (6%)
  local copies, waits for them, and re-layouts  2.65 us (4%)
    pallas_call x1, Pallas kernels, per_device(): pl.pallas_call(kernel, out_shape=(jax.ShapeDtypeStruct((1,), F32), jax.Sh...  66.5 us
    unnamed x2, local copies, waits for them, and re-layouts  2.65 us

profile of v2, /device:TPU:1, one launch (start us, length us, event | category | flops | bytes accessed | tf_op | source)
XLA Modules:
  0.0 73.9 jit_solution(13504590444713566864)
XLA Ops:
  1.3 66.5 %contrastive.1 = (f32[1]{0:T(128)}, f32[1]{0:T(128)}, f32[4,1024]{1,0:T(4,128)}, f32[4,1024]{1,0:T(4,128)}) custom-call(bf16[23,4,32,4,128]{4,3,2,1,0:T(4,128)(2,1)} %bitcast.4, f32[1,4096]{1,0:T(1,128)} %bitcast.5, bf16[4096,1024]{1,0:T(8,128)(2,1)} %in_weight.1, bf16[1024,1024]{1,0:T(8,128)(2,1)} %out_weight.1, bf16[4,1024]{1,0:T(4,128)(2,1)} %text.1, ...), custom_call_target="tpu_custom_call" | custom-call | tf_op jit(solution)/shard_map/contrastive/pallas_call | solution.py:450
  69.0 1.3 %copy.18 = f32[4,1024]{1,0:T(4,128)} copy(f32[4,1024]{1,0:T(4,128)} %get-tuple-element.10) | data formatting | bytes 32768
  70.3 1.3 %copy.19 = f32[4,1024]{1,0:T(4,128)} copy(f32[4,1024]{1,0:T(4,128)} %get-tuple-element.11) | data formatting | bytes 32768

commit v3 on v2

--- a/solution.py
+++ b/solution.py
@@ -14,6 +14,9 @@
 BF16 = jnp.bfloat16
 TOKENS, WIDE, E, HALF, ROWS = 92, 4096, 1024, 512, 1024
 BLOCKS = 23
+GROUPS = ((0, 8), (8, 8), (16, 7))
+LOG2E = 1.4426950408889634
+LN2 = 0.6931471805599453
 
 
 def coordinates():
@@ -209,16 +212,16 @@
     for b in range(NX * NY):
         column = jnp.sum(jnp.where(eye, jnp.broadcast_to(whole[b], (128, 128)), 0.0), axis=1, keepdims=True)
         for k in range(kinds):
-            out[k, b * 32 : b * 32 + 32, :] = column[k * 32 : k * 32 + 32]
+            out[k, b * 32 : b * 32 + 32, :] = jnp.broadcast_to(column[k * 32 : k * 32 + 32], (32, 128))
 
 
 def kernel(
-    images, gain, in_weight, out_weight, text, pair, scale,
+    images, gain_in, in_weight, out_weight, text_in, pair_in, scale_in,
     loss, norm, update_image, update_text,
-    pixels, normed, w, ow, pooled,
+    pixels, normed, w, ow, pooled, gain, text, pair, scale,
     text_send, text_line, text_all, image_send, image_line, image_all,
     tag_send, tag_line, tag_all, len_send, len_line, len_all,
-    scores, weights, row_lse, tags, lens, grad, own, swap_out, swap_in,
+    text_turned, turned_lse, scores, weights, row_high, row_part, row_lse, tags, lens, grad, own, swap_out, swap_in,
     load_sem, swap_sem, *sems,
 ):
     place = coordinates()
@@ -228,14 +231,24 @@
     tag_gather = SmallGather(place, tag_send, tag_line, tag_all, sems[16:22])
     len_gather = SmallGather(place, len_send, len_line, len_all, sems[22:28])
 
+    small = []
+    for i, (source, target) in enumerate(((text_in, text), (pair_in, pair), (gain_in, gain), (scale_in, scale))):
+        small.append(pltpu.make_async_copy(source, target, load_sem.at[i]))
+    pieces = []
+    for n, (start, size) in enumerate(GROUPS):
+        for i in range(4):
+            block = pl.ds(start, size)
+            pieces.append(
+                pltpu.make_async_copy(
+                    images.at[block, i], pixels.at[block, :, pl.ds(4 * i, 4)], load_sem.at[4 + 4 * n + i]
+                )
+            )
     loads = []
-    for i in range(4):
-        loads.append(pltpu.make_async_copy(images.at[:, i], pixels.at[:, :, pl.ds(4 * i, 4)], load_sem.at[i]))
     for n in range(4):
         part = pl.ds(n * 256, 256)
-        loads.append(pltpu.make_async_copy(in_weight.at[:, part], w.at[n], load_sem.at[4 + n]))
-    loads.append(pltpu.make_async_copy(out_weight, ow, load_sem.at[8]))
-    for copy in loads:
+        loads.append(pltpu.make_async_copy(in_weight.at[:, part], w.at[n], load_sem.at[16 + n]))
+    loads.append(pltpu.make_async_copy(out_weight, ow, load_sem.at[20]))
+    for copy in small + pieces + loads:
         copy.start()
 
     barrier = pltpu.get_barrier_semaphore()
@@ -250,6 +263,8 @@
     for where in peers:
         pl.semaphore_signal(barrier, inc=1, device_id=where, device_id_type=pl.DeviceIdType.MESH)
 
+    small[0].wait()
+    small[1].wait()
     text_unit, text_len = unit_rows(text[...].astype(F32))
     text_vec = text_unit.astype(BF16)
     for k in range(2):
@@ -263,41 +278,39 @@
         tag = tag + jnp.where(lane == first_lane + i, row.astype(F32), 0.0)
     tag_send[...] = tag
 
-    pl.semaphore_wait(barrier, len(peers))
-    text_gather.start_line()
-    tag_gather.start_line()
-
-    def normalise(i, carry):
+    def normalise(start, size):
         def tile(k):
-            return pixels[i, k].astype(F32)
-
-        total = jnp.zeros((16, 128), F32)
+            return pixels[start : start + size, k].astype(F32)
+
+        shift = jnp.sum(tile(0), axis=2, keepdims=True) * (1.0 / 128)
+        total = jnp.zeros((size, 16, 128), F32)
+        square = jnp.zeros((size, 16, 128), F32)
         for k in range(WIDE // 128):
-            total = total + tile(k)
-        average = jnp.sum(total, axis=1, keepdims=True) * (1.0 / WIDE)
-        total = jnp.zeros((16, 128), F32)
-        for k in range(WIDE // 128):
-            centered = tile(k) - average
-            total = total + centered * centered
-        variance = jnp.sum(total, axis=1, keepdims=True) * (1.0 / WIDE)
-        factor = lax.rsqrt(variance + EPS_LAYER)
+            moved = tile(k) - shift
+            total = total + moved
+            square = square + moved * moved
+        moved = jnp.sum(total, axis=2, keepdims=True) * (1.0 / WIDE)
+        variance = jnp.sum(square, axis=2, keepdims=True) * (1.0 / WIDE) - moved * moved
+        factor = lax.rsqrt(jnp.maximum(variance, 0.0) + EPS_LAYER)
+        average = shift + moved
         for k in range(WIDE // 128):
             part = slice(k * 128, (k + 1) * 128)
-            normed[i, :, part] = ((tile(k) - average) * factor * gain[:, part]).astype(BF16)
-        return carry
-
-    for i in range(4):
-        loads[i].wait()
-    lax.fori_loop(0, BLOCKS, normalise, 0)
-
-    text_gather.finish_line()
-    tag_gather.finish_line()
-    text_gather.start_second()
-    tag_gather.start_second()
+            normed[start : start + size, :, part] = ((tile(k) - average) * factor * gain[:, part]).astype(BF16)
+
+    small[2].wait()
+    small[3].wait()
+    for n, (start, size) in enumerate(GROUPS):
+        for copy in pieces[4 * n : 4 * n + 4]:
+            copy.wait()
+        if n == 1:
+            pl.semaphore_wait(barrier, len(peers))
+            text_gather.start_line()
+            tag_gather.start_line()
+        normalise(start, size)
 
     pooled[...] = jnp.zeros_like(pooled)
     for n in range(4):
-        loads[4 + n].wait()
+        loads[n].wait()
 
     def encode(n, carry):
         flat = normed[...].reshape(BLOCKS * 16, WIDE)
@@ -306,11 +319,13 @@
         pooled[n, 0:4, :] = (pairs[0:4] + pairs[4:8]) * (1.0 / TOKENS)
         return carry
 
-    lax.fori_loop(0, 2, encode, 0)
-    text_gather.finish_second()
-    tag_gather.finish_second()
-    lax.fori_loop(2, 4, encode, 0)
-    loads[8].wait()
+    lax.fori_loop(0, 3, encode, 0)
+    text_gather.finish_line()
+    tag_gather.finish_line()
+    text_gather.start_second()
+    tag_gather.start_second()
+    lax.fori_loop(3, 4, encode, 0)
+    loads[4].wait()
     image_emb = jnp.zeros((8, E), F32)
     for n in range(4):
         image_emb = image_emb + jnp.dot(
@@ -324,67 +339,95 @@
     image_gather.start_line()
     len_gather.start_line()
 
-    text_gather.finish_third()
-    tag_gather.finish_third()
-    columns_of(tag_all, tags, 4)
+    text_gather.finish_second()
+    tag_gather.finish_second()
     image_gather.finish_line()
     len_gather.finish_line()
     image_gather.start_second()
     len_gather.start_second()
-    text_gather.finish_cross()
+    text_gather.finish_third()
+    tag_gather.finish_third()
     image_gather.finish_second()
     len_gather.finish_second()
+    text_gather.finish_cross()
+    columns_of(tag_all, tags, 4)
+    for k in range(2):
+        for n in range(8):
+            rows = text_all[k].reshape(ROWS, HALF)[n * 128 : (n + 1) * 128]
+            text_turned[k, :, n * 128 : (n + 1) * 128] = rows.T
     image_gather.finish_third()
     len_gather.finish_third()
+    columns_of(len_all, lens, 2)
     image_gather.finish_cross()
-    columns_of(len_all, lens, 2)
 
     multiplier = scale[0]
-
-    def score(chunk, carry):
-        side, b = chunk // 2, (chunk % 2) * 8
+    high = jnp.full((8, ROWS), -jnp.inf, F32)
+    for n in range(4):
+        side, b = n // 2, (n % 2) * 8
         total = jnp.zeros((256, ROWS), F32)
         for k in range(2):
-            total = total + lax.dot_general(
-                image_all[k, side, pl.ds(b, 8)].reshape(256, HALF),
-                text_all[k].reshape(ROWS, HALF),
-                (((1,), (1,)), ((), ())),
-                preferred_element_type=F32,
-            )
-        scores[pl.ds(pl.multiple_of(chunk * 256, 256), 256), :] = total * multiplier
+            vectors = image_all[k, side, b : b + 8].reshape(256, HALF)
+            total = total + jnp.dot(vectors, text_turned[k], preferred_element_type=F32)
+        total = total * (multiplier * LOG2E)
+        rows = slice(n * 256, (n + 1) * 256)
+        scores[rows, :] = total
+        top = total[:, 0:128]
+        for t in range(1, 8):
+            top = jnp.maximum(top, total[:, t * 128 : (t + 1) * 128])
+        row_high[rows, :] = jnp.broadcast_to(jnp.max(top, axis=1, keepdims=True), (256, 128))
+        high = jnp.maximum(high, jnp.max(total.reshape(32, 8, ROWS), axis=0))
+    high = jnp.max(high, axis=0, keepdims=True)
+
+    def sums(r, total):
+        rows = pl.ds(pl.multiple_of(r * 32, 32), 32)
+        top = row_high[rows, :]
+        part = jnp.zeros((32, 128), F32)
+        down = []
+        for t in range(8):
+            lanes = slice(t * 128, (t + 1) * 128)
+            s = scores[rows, lanes]
+            part = part + jnp.exp2(s - top)
+            down.append(jnp.sum(jnp.exp2(s - high[:, lanes]).reshape(4, 8, 128), axis=0))
+        row_part[rows, :] = part
+        return total + jnp.concatenate(down, axis=1)
+
+    total = lax.fori_loop(0, 32, sums, jnp.zeros((8, ROWS), F32))
+    col_lse = high + jnp.log2(jnp.sum(total, axis=0, keepdims=True))
+    row_sum = jnp.sum(row_part[...], axis=1, keepdims=True)
+    row_lse[...] = row_high[...] + jnp.log2(jnp.broadcast_to(row_sum, (ROWS, 128)))
+
+    lane = lax.broadcasted_iota(jnp.int32, (1, 128), 1).astype(F32)
+
+    def weigh_own(r, positive):
+        at = pl.multiple_of(r * 32, 32)
+        rows = pl.ds(pl.multiple_of(c * HALF + at, 32), 32)
+        tag, lse = tags[c, pl.ds(at, 32), :], row_lse[rows, :]
+        for t in range(8):
+            lanes = slice(t * 128, (t + 1) * 128)
+            s = scores[rows, lanes]
+            hit = tag == lane + (t * 128.0)
+            value = jnp.exp2(s - lse) + jnp.exp2(s - col_lse[:, lanes]) - jnp.where(hit, 2.0, 0.0)
+            weights[c, pl.ds(at, 32), lanes] = value.astype(BF16)
+            positive = positive + jnp.where(hit, s, 0.0)
+        return positive
+
+    positive = lax.fori_loop(0, 16, weigh_own, jnp.zeros((32, 128), F32))
+    turned_lse[...] = col_lse
+    d = 1 - c
+
+    def weigh_other(r, carry):
+        at = pl.multiple_of(r * 32, 32)
+        rows = pl.ds(pl.multiple_of(d * HALF + at, 32), 32)
+        tag, lse = tags[d, pl.ds(at, 32), :] - (c * HALF).astype(F32), row_lse[rows, :]
+        for t in range(4):
+            lanes = pl.ds(pl.multiple_of(c * HALF + t * 128, 128), 128)
+            s = scores[rows, lanes]
+            hit = tag == lane + (t * 128.0)
+            value = jnp.exp2(s - lse) + jnp.exp2(s - turned_lse[:, lanes]) - jnp.where(hit, 2.0, 0.0)
+            weights[d, pl.ds(at, 32), lanes] = value.astype(BF16)
         return carry
 
-    lax.fori_loop(0, 4, score, 0)
-
-    def over_rows(r, high):
-        rows = pl.ds(pl.multiple_of(r * 32, 32), 32)
-        s = scores[rows, :]
-        top = jnp.max(s, axis=1, keepdims=True)
-        row_lse[rows, :] = top + jnp.log(jnp.sum(jnp.exp(s - top), axis=1, keepdims=True))
-        return jnp.maximum(high, jnp.max(s.reshape(4, 8, ROWS), axis=0))
-
-    high = lax.fori_loop(0, 32, over_rows, jnp.full((8, ROWS), -jnp.inf, F32))
-    high = jnp.max(high, axis=0, keepdims=True)
-
-    def over_columns(r, total):
-        rows = pl.ds(pl.multiple_of(r * 32, 32), 32)
-        return total + jnp.sum(jnp.exp(scores[rows, :] - high).reshape(4, 8, ROWS), axis=0)
-
-    total = lax.fori_loop(0, 32, over_columns, jnp.zeros((8, ROWS), F32))
-    col_lse = high + jnp.log(jnp.sum(total, axis=0, keepdims=True))
-
-    ids = lax.broadcasted_iota(jnp.int32, (32, ROWS), 1).astype(F32)
-
-    def weigh(r, positive):
-        rows = pl.ds(pl.multiple_of(r * 32, 32), 32)
-        s = scores[rows, :]
-        hit = ids == tags[r // 16, pl.ds(pl.multiple_of((r % 16) * 32, 32), 32), :]
-        value = jnp.exp(s - row_lse[rows, :]) + jnp.exp(s - col_lse) - jnp.where(hit, 2.0, 0.0)
-        weights[r // 16, pl.ds(pl.multiple_of((r % 16) * 32, 32), 32), :] = value.astype(BF16)
-        return positive + jnp.sum(jnp.where(hit, s, 0.0).reshape(4, 8, ROWS), axis=0)
-
-    positive = lax.fori_loop(0, 32, weigh, jnp.zeros((8, ROWS), F32))
-    loss[0] = (jnp.sum(row_lse[...]) + jnp.sum(col_lse) - 2.0 * jnp.sum(positive)) * (0.5 / ROWS)
+    lax.fori_loop(0, 16, weigh_other, 0)
 
     squares = jnp.zeros((HALF, 1), F32)
     b = x * NY + y
@@ -410,11 +453,12 @@
             u = vectors[k, c].reshape(HALF, HALF).astype(F32)
             size = size + jnp.sum(g * g, axis=1, keepdims=True)
             along = along + jnp.sum(g * u, axis=1, keepdims=True)
-        length = lens[c] if side == 0 else tags[2 + c]
+        length = lens[c, :, 0:1] if side == 0 else tags[2 + c, :, 0:1]
         inverse = 1.0 / (length * length)
         squares = squares + (size - along * along * (1.0 + EPS_UNIT * inverse)) * inverse
 
-    swap_out[...] = jnp.broadcast_to(jnp.sum(squares, axis=0, keepdims=True), (8, 128))
+    swap_out[0] = jnp.broadcast_to(jnp.sum(squares, axis=0, keepdims=True), (8, 128))
+    swap_out[1] = jnp.broadcast_to(jnp.sum(jnp.sum(positive, axis=0, keepdims=True), axis=1, keepdims=True), (8, 128))
     swap = remote(swap_out, swap_in, swap_sem.at[0], swap_sem.at[1], (z, x, y, 1 - c))
     swap.start()
 
@@ -423,12 +467,14 @@
 
     grad_image = own_gradient(own[0], image_unit, image_len)
     grad_text = own_gradient(own[1], text_unit, text_len)
+    spread_lse = jnp.sum(row_lse[...]) * (1.0 / 128) + jnp.sum(col_lse)
     swap.wait_recv()
-    total = swap_out[...] + swap_in[...]
-    factor = lax.rsqrt(total[0:1, 0:1] * (1.0 / (2.0 * ROWS * E)) + 1e-06)
+    total = (swap_out[0] + swap_in[0])[0:1, 0:1]
+    factor = lax.rsqrt(total * (1.0 / (2.0 * ROWS * E)) + 1e-06)
     update_image[...] = grad_image * factor
     update_text[...] = grad_text * factor
-    norm[0] = jnp.sqrt(jnp.sum(total) * (1.0 / (8.0 * 128.0)))
+    norm[0] = jnp.sum(jnp.sqrt(total))
+    loss[0] = (spread_lse - 2.0 * jnp.sum((swap_out[1] + swap_in[1])[0:1, 0:1])) * (LN2 * 0.5 / ROWS)
     swap.wait_send()
     for gather in (text_gather, tag_gather, image_gather, len_gather):
         gather.drain()
@@ -455,7 +501,7 @@
             jax.ShapeDtypeStruct((4, E), F32),
             jax.ShapeDtypeStruct((4, E), F32),
         ),
-        in_specs=[any_space, vmem, any_space, any_space, vmem, smem, smem],
+        in_specs=[any_space] * 7,
         out_specs=(smem, smem, vmem, vmem),
         scratch_shapes=[
             pltpu.VMEM((BLOCKS, WIDE // 128, 16, 128), BF16),
@@ -463,20 +509,28 @@
             pltpu.VMEM((4, WIDE, 256), BF16),
             pltpu.VMEM((E, E), BF16),
             pltpu.VMEM((4, 8, 256), F32),
+            pltpu.VMEM((1, WIDE), F32),
+            pltpu.VMEM((4, E), BF16),
+            pltpu.SMEM((4,), jnp.int32),
+            pltpu.SMEM((1,), F32),
             *matrix,
             *matrix,
             *lanes,
             *lanes,
+            pltpu.VMEM((2, HALF, ROWS), BF16),
+            pltpu.VMEM((1, ROWS), F32),
             pltpu.VMEM((ROWS, ROWS), F32),
             pltpu.VMEM((2, HALF, ROWS), BF16),
-            pltpu.VMEM((ROWS, 1), F32),
-            pltpu.VMEM((4, HALF, 1), F32),
-            pltpu.VMEM((2, HALF, 1), F32),
+            pltpu.VMEM((ROWS, 128), F32),
+            pltpu.VMEM((ROWS, 128), F32),
+            pltpu.VMEM((ROWS, 128), F32),
+            pltpu.VMEM((4, HALF, 128), F32),
+            pltpu.VMEM((2, HALF, 128), F32),
             pltpu.VMEM((NX * NY, 32, HALF), F32),
             pltpu.VMEM((2, 4, E), F32),
-            pltpu.VMEM((8, 128), F32),
-            pltpu.VMEM((8, 128), F32),
-            dma((9,)),
+            pltpu.VMEM((2, 8, 128), F32),
+            pltpu.VMEM((2, 8, 128), F32),
+            dma((21,)),
             dma((2,)),
             *big,
             *big,

time: 74.3 us -> 60.9 us (0.82)
  Pallas kernels: 66.5 us -> 53 us
    pallas_call x1, Pallas kernels: 66.5 us -> 53 us  [per_device(): pl.pallas_call(kernel, out_shape=(jax.ShapeDtypeStruct((1,), F32), jax.Sh...]
where the time goes in v3:
time: 60.9 us; the launch traced here: 60.4 us
  Pallas kernels  53 us (87%)
  between operations  4.78 us (8%)
  local copies, waits for them, and re-layouts  2.65 us (4%)
    pallas_call x1, Pallas kernels, per_device(): pl.pallas_call(kernel, out_shape=(jax.ShapeDtypeStruct((1,), F32), jax.Sh...  53 us
    unnamed x2, local copies, waits for them, and re-layouts  2.65 us

profile of v3, /device:TPU:1, one launch (start us, length us, event | category | flops | bytes accessed | tf_op | source)
XLA Modules:
  0.0 60.4 jit_solution(2449686085959784960)
XLA Ops:
  1.3 53.0 %contrastive.1 = (f32[1]{0:T(128)}, f32[1]{0:T(128)}, f32[4,1024]{1,0:T(4,128)}, f32[4,1024]{1,0:T(4,128)}) custom-call(bf16[23,4,32,4,128]{4,3,2,1,0:T(4,128)(2,1)} %bitcast.4, f32[1,4096]{1,0:T(1,128)} %bitcast.5, bf16[4096,1024]{1,0:T(8,128)(2,1)} %in_weight.1, bf16[1024,1024]{1,0:T(8,128)(2,1)} %out_weight.1, bf16[4,1024]{1,0:T(4,128)(2,1)} %text_in.1, ...), custom_call_target="tpu_custom_call" | custom-call | tf_op jit(solution)/shard_map/contrastive/pallas_call | solution.py:496
  55.5 1.3 %copy.18 = f32[4,1024]{1,0:T(4,128)} copy(f32[4,1024]{1,0:T(4,128)} %get-tuple-element.10) | data formatting | bytes 32768
  56.9 1.3 %copy.19 = f32[4,1024]{1,0:T(4,128)} copy(f32[4,1024]{1,0:T(4,128)} %get-tuple-element.11) | data formatting | bytes 32768
